TPU v7x, 256 devices: a whole 4x4x8 slice. The times are simulated.
256 devices in a mesh: replica: 64 (over z, x, core), model: 4 (over y).
Axes of the slice: x: 4, y: 4, z: 8, core: 2. Of those that a mesh axis runs over, the one named last changes fastest.
Arguments:
- partial_query: float32 [64, 1280, 1280], P('replica', None, 'model'), may hold values from -1.75 to 1.75
- partial_key: float32 [64, 1280, 1280], P('replica', None, 'model'), may hold values from -1.75 to 1.75
- partial_value: float32 [64, 1280, 1280], P('replica', None, 'model'), may hold values from -1.75 to 1.75
- partial_mixed: float32 [64, 1280, 1280], P('replica', 'model'), may hold values from -1.75 to 1.75
- partial_norm: float32 [64, 1280], P('replica'), may hold values from -16 to 16
- master_query: float32 [1280, 1280], P('replica', 'model'), may hold values from -0.15625 to 0.15625
- master_key: float32 [1280, 1280], P('replica', 'model'), may hold values from -0.15625 to 0.15625
- master_value: float32 [1280, 1280], P('replica', 'model'), may hold values from -0.15625 to 0.15625
- master_mixed: float32 [1280, 1280], P('model', 'replica'), may hold values from -0.15625 to 0.15625
- master_norm: float32 [1280], P('replica'), may hold values from 0.25 to 1.75
Outputs:
- compute_query: bfloat16 [1280, 1280], P(None, 'model')
- compute_key: bfloat16 [1280, 1280], P(None, 'model')
- compute_value: bfloat16 [1280, 1280], P(None, 'model')
- compute_mixed: bfloat16 [1280, 1280], P('model')
- compute_norm: bfloat16 [1280], replicated
- stepped_query: float32 [1280, 1280], P('replica', 'model')
- stepped_key: float32 [1280, 1280], P('replica', 'model')
- stepped_value: float32 [1280, 1280], P('replica', 'model')
- stepped_mixed: float32 [1280, 1280], P('model', 'replica')
- stepped_norm: float32 [1280], P('replica')
All inputs are finite; a program needn't handle non-finite values.
Results may differ from a plain program's by a relative error of at most 0.001.
Values may be sent and summed in bfloat16 or wider, within the bound.
No kernel may reach another device: no remote copies, remote signals or barrier semaphores. Data moves between devices by JAX's collectives and lax.ppermute only.
A program may use at most 128 MiB of HBM per device.

v0:
```python
import jax
import jax.numpy as jnp
from jax import lax
from jax.sharding import PartitionSpec as P

learn_rate = 0.3


def cut_along(x, dim, peers):
    before, after = (x.shape[:dim], x.shape[dim + 1 :])
    return jnp.moveaxis(x.reshape(*before, peers, -1, *after), dim, 0)


def sum_together(arrays, axis, dims):
    peers = lax.axis_size(axis)
    parts = [cut_along(a, dim, peers) for a, dim in zip(arrays, dims)]
    lines = jnp.concatenate([b.reshape(peers, -1) for b in parts], axis=1)
    extent = max(16, -(-lines.shape[1] // 1024) * 8)
    lines = jnp.pad(lines, ((0, 0), (0, extent * 128 - lines.shape[1]))).reshape(-1, 128)
    flat, at, finished = (lax.psum_scatter(lines, axis, tiled=True).reshape(-1), 0, [])
    for b in parts:
        part = b[0]
        finished.append(flat[at : at + part.size].reshape(part.shape))
        at += part.size
    return tuple(finished)


def gathered_total(x, axis):
    parts = lax.all_gather(x, axis)
    return parts.sum(axis=0)


def gather_turned(arrays, axis, dims):
    turned = [jnp.moveaxis(a, dim, 0) for a, dim in zip(arrays, dims)]
    both = jnp.concatenate([t.reshape(len(t), -1) for t in turned], axis=1)
    filled, at, finished = (lax.all_gather(both, axis, axis=0, tiled=True), 0, [])
    for t, dim in zip(turned, dims):
        share = filled[:, at : at + t[0].size].reshape(-1, *t.shape[1:])
        finished.append(jnp.moveaxis(share, 0, dim))
        at += t[0].size
    return tuple(finished)


def on_device(
    partial_query,
    partial_key,
    partial_value,
    partial_mixed,
    partial_norm,
    master_query,
    master_key,
    master_value,
    master_mixed,
    master_norm,
):
    mean_query, mean_key, mean_value, mean_mixed = sum_together(
        (partial_query[0], partial_key[0], partial_value[0], partial_mixed[0]),
        "replica",
        (0, 0, 0, 1),
    )
    whole_norm = gathered_total(partial_norm[0], "replica")
    place = lax.axis_index("replica")
    mean_norm = lax.dynamic_slice_in_dim(
        whole_norm, place * master_norm.shape[0], master_norm.shape[0]
    )
    mean_rate = lax.axis_size("replica") ** (-0.5)
    mean_query = mean_query * mean_rate
    mean_key = mean_key * mean_rate
    mean_value = mean_value * mean_rate
    mean_mixed = mean_mixed * mean_rate
    mean_norm = mean_norm * mean_rate
    stepped_query = master_query - learn_rate * mean_query
    stepped_key = master_key - learn_rate * mean_key
    stepped_value = master_value - learn_rate * mean_value
    stepped_mixed = master_mixed - learn_rate * mean_mixed
    stepped_norm = master_norm - learn_rate * mean_norm
    compute_query, compute_key, compute_value, compute_mixed, compute_norm = gather_turned(
        (
            stepped_query.astype(jnp.bfloat16),
            stepped_key.astype(jnp.bfloat16),
            stepped_value.astype(jnp.bfloat16),
            stepped_mixed.astype(jnp.bfloat16),
            stepped_norm.astype(jnp.bfloat16),
        ),
        "replica",
        (0, 0, 0, 1, 0),
    )
    return (
        compute_query,
        compute_key,
        compute_value,
        compute_mixed,
        compute_norm,
        stepped_query,
        stepped_key,
        stepped_value,
        stepped_mixed,
        stepped_norm,
    )


def solution(mesh):
    in_specs = (
        P("replica", None, "model"),
        P("replica", None, "model"),
        P("replica", None, "model"),
        P("replica", "model", None),
        P("replica", None),
        P("replica", "model"),
        P("replica", "model"),
        P("replica", "model"),
        P("model", "replica"),
        P("replica"),
    )
    out_specs = (
        P(None, "model"),
        P(None, "model"),
        P(None, "model"),
        P("model", None),
        P(),
        P("replica", "model"),
        P("replica", "model"),
        P("replica", "model"),
        P("model", "replica"),
        P("replica"),
    )
    return jax.shard_map(
        on_device, mesh=mesh, in_specs=in_specs, out_specs=out_specs, check_vma=False
    )
```

profile of v0, /device:TPU:1, one launch (start us, length us, event | category | flops | bytes accessed | tf_op | source)
XLA Modules:
  0.0 357.2 jit_solution(15330442983936035255)
XLA Ops:
  7.2 0.0 all-reduce.3.cloned.1.call-start
  7.2 2.8 copy.59
  10.1 1.6 reshape_squeeze.3
  11.7 3.2 copy.60
  14.9 2.8 reshape.53
  17.8 2.1 copy.61
  19.9 1.8 copy.58
  21.7 2.2 reshape_reshape_squeeze.11
  24.0 1.8 copy.57
  25.8 2.1 reshape_reshape_squeeze.10
  27.9 1.8 copy.56
  29.8 2.2 reshape_reshape_squeeze.9
  32.0 4.8 %pad_maximum_fusion = f32[64,25600]{1,0:T(8,128)} fusion(f32[64,6400]{1,0:T(8,128)} %copy.61, f32[64,6400]{1,0:T(8,128)} %reshape_reshape_squeeze.11, f32[64,6400]{1,0:T(8,128)} %reshape_reshape_squeeze.10, f32[64,6400]{1,0:T(8,128)} %reshape_reshape_squeeze.9), kind=kLoop, calls=%fused_computation | loop fusion | flops 4915200 | bytes 13107200 | tf_op jit(solution)/shard_map/concatenate | solution.py:17
  36.8 6.4 %reshape.54 = f32[12800,128]{1,0:T(8,128)} reshape(f32[64,25600]{1,0:T(8,128)} %pad_maximum_fusion) | data formatting | bytes 13107200 | tf_op jit(solution)/shard_map/reshape | solution.py:19
  43.2 0.0 copy-start.6
  43.2 0.0 copy-start.4
  43.2 0.0 copy-start.5
  43.2 0.0 copy-start
  43.2 0.0 copy-start.1
  43.2 0.0 copy-start.2
  43.2 0.0 copy-start.3
  43.2 0.0 all-reduce.3.cloned.1.call-update
  43.2 0.0 all-gather.4.cloned.1.call-start
  43.3 0.5 copy-done.6
  43.8 0.6 dynamic-slice
  45.1 0.0 copy-done.4
  45.1 53.4 %all-gather = f32[64,1,1280]{2,1,0:T(1,128)S(1)} all-gather(f32[1,1,1280]{2,1,0:T(1,128)S(1)} %bitcast.16), channel_id=1, replica_groups=mesh['replica'=64,'model'=4] {'replica'}, dimensions={0}, use_global_device_ids=true | all-gather | bytes 332800 | tf_op jit(solution)/shard_map/all_gather | solution.py:29
  98.5 0.2 reduce_sum.9
  98.7 0.0 copy-done.5
  98.7 0.6 convert_bitcast_fusion.1
  99.3 0.1 copy.63
  99.4 147.8 %all-reduce.3.cloned.1.call-done = f32[12800,128]{1,0:T(8,128)} async-done(((f32[12800,128]{1,0:T(8,128)}), f32[12800,128]{1,0:T(8,128)}) %all-reduce.3.cloned.1.call-update) | async-done | bytes 6553616
  247.1 0.9 dynamic-slice_multiply_fusion
  248.0 0.1 mul.43
  248.1 0.1 mul.47
  248.2 0.1 mul.45
  248.2 0.2 mul.49
  248.4 0.1 copy.62
  248.5 0.0 copy-done
  248.5 0.6 fusion.2
  249.2 0.0 copy-done.1
  249.2 0.6 convert_bitcast_fusion
  249.8 0.0 copy-done.2
  249.8 0.0 copy-done.3
  249.8 0.6 fusion
  250.4 0.7 concatenate.7
  251.2 0.0 all-gather.4.cloned.1.call-update
  251.2 80.2 %all-gather.4.cloned.1.call-done = bf16[64,20,1281]{2,1,0:T(8,128)(2,1)} async-done(((bf16[1,20,1281]{2,1,0:T(8,128)(2,1)}), bf16[64,20,1281]{2,1,0:T(8,128)(2,1)}) %all-gather.4.cloned.1.call-update) | async-done | bytes 3279376 | tf_op jit(solution)/shard_map/all_gather | solution.py:36
  331.4 6.8 %reshape.60 = bf16[1280,1281]{1,0:T(8,128)(2,1)} reshape(bf16[64,20,1281]{2,1,0:T(8,128)(2,1)} %all-gather.4.cloned.1.call-done) | data formatting | bytes 6558720
  338.2 4.5 %slice_bitcast_fusion = (bf16[320,1280]{0,1:T(8,128)(2,1)S(1)}, bf16[1280,320]{1,0:T(8,128)(2,1)S(1)}, bf16[1280,320]{1,0:T(8,128)(2,1)S(1)}, bf16[1280,320]{1,0:T(8,128)(2,1)}) fusion(bf16[1280,1281]{1,0:T(8,128)(2,1)} %reshape.60), kind=kLoop, calls=%fused_computation.1 | loop fusion | bytes 6553600 | tf_op jit(solution)/shard_map/transpose | solution.py:39
  342.6 1.7 slice_reduce_fusion
  344.4 2.2 copy.64
  346.5 1.3 copy.65
  347.8 1.3 copy.66
  349.1 1.3 copy.67
Async XLA Ops:
  7.2 240.0 %all-reduce.3.cloned.1.call-start = ((), (), s32[]{:S(2)}) async-start(), calls=%async_computation.1 | async-start | bytes 13107200
  43.2 0.7 copy-start.6
  43.2 1.9 copy-start.4
  43.2 55.5 %copy-start.5 = (f32[20]{0:T(128)S(1)}, f32[20]{0:T(128)}, u32[]{:S(2)}) copy-start(f32[20]{0:T(128)} %param.19) | copy-start | bytes 244
  43.2 205.4 %copy-start = (f32[20,320]{1,0:T(8,128)S(1)}, f32[20,320]{1,0:T(8,128)}, u32[]{:S(2)}) copy-start(f32[20,320]{1,0:T(8,128)} %param.15) | copy-start | bytes 76804
  43.2 206.0 %copy-start.1 = (f32[320,20]{0,1:T(8,128)S(1)}, f32[320,20]{0,1:T(8,128)}, u32[]{:S(2)}) copy-start(f32[320,20]{0,1:T(8,128)} %param.18) | copy-start | bytes 76804
  43.2 206.6 %copy-start.2 = (f32[20,320]{1,0:T(8,128)S(1)}, f32[20,320]{1,0:T(8,128)}, u32[]{:S(2)}) copy-start(f32[20,320]{1,0:T(8,128)} %param.17) | copy-start | bytes 76804
  43.2 206.6 %copy-start.3 = (f32[20,320]{1,0:T(8,128)S(1)}, f32[20,320]{1,0:T(8,128)}, u32[]{:S(2)}) copy-start(f32[20,320]{1,0:T(8,128)} %param.16) | copy-start | bytes 76804
  43.2 288.1 %all-gather.4.cloned.1.call-start = ((), (), s32[]{:S(2)}) async-start(), calls=%async_computation | async-start | bytes 4392960 | tf_op jit(solution)/shard_map/all_gather | solution.py:36
Sparse Core Ops, SparseCore 0:
  43.4 203.7 all-reduce.2
  251.3 79.9 all-gather.3
where the time goes:
time: 358 us; the launch traced here: 357 us
  waiting for transfers between devices  228 us (64%)
  blocking collectives  53.4 us (15%)
  local copies, waits for them, and re-layouts  52.5 us (15%)
  between operations  14.8 us (4%)
  other arithmetic  8.4 us (2%)
    unnamed x3, waiting for transfers between devices  148 us
    all_gather x1, waiting for transfers between devices, gather_turned(): lax.all_gather(both, axis, axis=0, tiled=True)  80.2 us
    all_gather x1, blocking collectives, gathered_total(): parts = lax.all_gather(x, axis)  53.4 us
    unnamed x24, local copies, waits for them, and re-layouts  22.2 us
  transfers between devices with their start and end apart: 2, of which 2 were waited for; matrix products, arithmetic and copies ran while one was open for 0% of the time, Pallas kernels for 0%

commit v1 on v0

--- a/solution.py
+++ b/solution.py
@@ -33,7 +33,13 @@
 def gather_turned(arrays, axis, dims):
     turned = [jnp.moveaxis(a, dim, 0) for a, dim in zip(arrays, dims)]
     both = jnp.concatenate([t.reshape(len(t), -1) for t in turned], axis=1)
-    filled, at, finished = (lax.all_gather(both, axis, axis=0, tiled=True), 0, [])
+    filled, at, finished = (
+        jnp.concatenate(
+            lax.all_to_all(jnp.stack([both] * lax.axis_size(axis)), axis, 0, 0), axis=0
+        ),
+        0,
+        [],
+    )
     for t, dim in zip(turned, dims):
         share = filled[:, at : at + t[0].size].reshape(-1, *t.shape[1:])
         finished.append(jnp.moveaxis(share, 0, dim))

time: 358 us -> 388 us (1.084)
  blocking collectives: 53.4 us -> 164 us
  waiting for transfers between devices: 228 us -> 148 us
    all_to_all x0 -> x1, blocking collectives: none -> 111 us  [gather_turned(): lax.all_to_all(jnp.stack([both] * lax.axis_size(axis)), axis, 0, 0)]
    all_gather x1 -> x0, waiting for transfers between devices: 80.2 us -> none  [gather_turned(): lax.all_gather(both, axis, axis=0, tiled=True)]
    reshape x0 -> x1, local copies, waits for them, and re-layouts: none -> 6.79 us  [gather_turned(): jnp.concatenate(lax.all_to_all(jnp.stack([both] * lax.axis_size(axis)), a...]
    unnamed x24 -> x23, local copies, waits for them, and re-layouts: 22.2 us -> 15.5 us
    unnamed x3 -> x2, waiting for transfers between devices: 148 us -> 148 us
  transfers between devices with their start and end apart: 2 -> 1, of which waited for: 2 -> 1; matrix products, arithmetic and copies ran while one was open for 0% -> 0% of each run, Pallas kernels for 0% -> 0%
where the time goes in v1:
time: 388 us
  blocking collectives  164 us (42%)
  waiting for transfers between devices  148 us (38%)
  local copies, waits for them, and re-layouts  52.2 us (13%)
  between operations  14.8 us (4%)
  other arithmetic  8.4 us (2%)
    unnamed x2, waiting for transfers between devices  148 us
    all_to_all x1, blocking collectives, gather_turned(): lax.all_to_all(jnp.stack([both] * lax.axis_size(axis)), axis, 0, 0)  111 us
    all_gather x1, blocking collectives, gathered_total(): parts = lax.all_gather(x, axis)  53.4 us
    unnamed x23, local copies, waits for them, and re-layouts  15.5 us
  transfers between devices with their start and end apart: 1, of which 1 were waited for; matrix products, arithmetic and copies ran while one was open for 0% of the time, Pallas kernels for 0%

profile of v1, /device:TPU:1, one launch (start us, length us, event | category | flops | bytes accessed | tf_op | source)
XLA Modules:
  0.0 387.6 jit_solution(17960639999276861835)
XLA Ops:
  7.2 0.0 all-reduce.3.cloned.1.call-start
  7.2 2.8 copy.56
  10.1 1.6 reshape_squeeze.3
  11.7 3.3 copy.57
  14.9 2.8 reshape.58
  17.8 2.1 copy.58
  19.9 1.8 copy.55
  21.8 2.2 reshape_reshape_squeeze.11
  24.0 1.8 copy.54
  25.8 2.1 reshape_reshape_squeeze.10
  27.9 1.8 copy.53
  29.8 2.2 reshape_reshape_squeeze.9
  32.0 4.8 %pad_maximum_fusion = f32[64,25600]{1,0:T(8,128)} fusion(f32[64,6400]{1,0:T(8,128)} %copy.58, f32[64,6400]{1,0:T(8,128)} %reshape_reshape_squeeze.11, f32[64,6400]{1,0:T(8,128)} %reshape_reshape_squeeze.10, f32[64,6400]{1,0:T(8,128)} %reshape_reshape_squeeze.9), kind=kLoop, calls=%fused_computation | loop fusion | flops 4915200 | bytes 13107200 | tf_op jit(solution)/shard_map/concatenate | solution.py:17
  36.8 6.3 %reshape.59 = f32[12800,128]{1,0:T(8,128)} reshape(f32[64,25600]{1,0:T(8,128)} %pad_maximum_fusion) | data formatting | bytes 13107200 | tf_op jit(solution)/shard_map/reshape | solution.py:19
  43.1 0.0 copy-start.6
  43.1 0.0 copy-start.4
  43.1 0.0 copy-start.5
  43.1 0.0 copy-start
  43.1 0.0 copy-start.1
  43.1 0.0 copy-start.2
  43.2 0.0 copy-start.3
  43.2 0.0 all-reduce.3.cloned.1.call-update
  43.2 0.6 copy-done.6
  43.8 0.6 dynamic-slice
  45.0 0.0 copy-done.4
  45.0 53.4 %all-gather = f32[64,1,1280]{2,1,0:T(1,128)S(1)} all-gather(f32[1,1,1280]{2,1,0:T(1,128)S(1)} %bitcast.14), channel_id=1, replica_groups=mesh['replica'=64,'model'=4] {'replica'}, dimensions={0}, use_global_device_ids=true | all-gather | bytes 332800 | tf_op jit(solution)/shard_map/all_gather | solution.py:29
  98.4 0.2 reduce_sum.9
  98.6 0.0 copy-done.5
  98.6 0.6 convert_bitcast_fusion.1
  99.2 0.1 copy.60
  99.3 147.8 %all-reduce.3.cloned.1.call-done = f32[12800,128]{1,0:T(8,128)} async-done(((f32[12800,128]{1,0:T(8,128)}), f32[12800,128]{1,0:T(8,128)}) %all-reduce.3.cloned.1.call-update) | async-done | bytes 6553616
  247.1 0.9 dynamic-slice_multiply_fusion
  248.0 0.1 mul.43
  248.0 0.1 mul.47
  248.1 0.1 mul.45
  248.2 0.2 mul.49
  248.4 0.1 copy.59
  248.5 0.0 copy-done
  248.5 0.6 fusion.2
  249.1 0.0 copy-done.1
  249.1 0.6 convert_bitcast_fusion
  249.8 0.0 copy-done.2
  249.8 0.0 copy-done.3
  249.8 0.6 fusion
  250.4 0.1 concatenate.7
  250.5 0.3 stack.2
  250.8 111.0 %all_to_all.5 = bf16[64,20,1281]{2,1,0:T(8,128)(2,1)} all-to-all(bf16[64,20,1281]{2,1,0:T(8,128)(2,1)S(1)} %stack.2), channel_id=1, replica_groups=mesh['replica'=64,'model'=4] {'replica'}, dimensions={0} | all-to-all | bytes 6558720 | tf_op jit(solution)/shard_map/all_to_all | solution.py:38
  361.8 6.8 %reshape.61 = bf16[1280,1281]{1,0:T(8,128)(2,1)} reshape(bf16[64,20,1281]{2,1,0:T(8,128)(2,1)} %all_to_all.5) | data formatting | bytes 6558720 | tf_op jit(solution)/shard_map/reshape | solution.py:37
  368.6 4.5 %slice_bitcast_fusion = (bf16[320,1280]{0,1:T(8,128)(2,1)S(1)}, bf16[1280,320]{1,0:T(8,128)(2,1)S(1)}, bf16[1280,320]{1,0:T(8,128)(2,1)S(1)}, bf16[1280,320]{1,0:T(8,128)(2,1)}) fusion(bf16[1280,1281]{1,0:T(8,128)(2,1)} %reshape.61), kind=kLoop, calls=%fused_computation.1 | loop fusion | bytes 6553600 | tf_op jit(solution)/shard_map/transpose | solution.py:45
  373.0 1.7 slice_reduce_fusion
  374.8 2.2 copy.61
  376.9 1.3 copy.62
  378.2 1.3 copy.63
  379.5 1.3 copy.64
Async XLA Ops:
  7.2 239.9 %all-reduce.3.cloned.1.call-start = ((), (), s32[]{:S(2)}) async-start(), calls=%async_computation.1 | async-start | bytes 13107200
  43.1 0.7 copy-start.6
  43.1 1.9 copy-start.4
  43.1 55.5 %copy-start.5 = (f32[20]{0:T(128)S(1)}, f32[20]{0:T(128)}, u32[]{:S(2)}) copy-start(f32[20]{0:T(128)} %param.19) | copy-start | bytes 244
  43.1 205.4 %copy-start = (f32[20,320]{1,0:T(8,128)S(1)}, f32[20,320]{1,0:T(8,128)}, u32[]{:S(2)}) copy-start(f32[20,320]{1,0:T(8,128)} %param.15) | copy-start | bytes 76804
  43.1 206.0 %copy-start.1 = (f32[320,20]{0,1:T(8,128)S(1)}, f32[320,20]{0,1:T(8,128)}, u32[]{:S(2)}) copy-start(f32[320,20]{0,1:T(8,128)} %param.18) | copy-start | bytes 76804
  43.1 206.6 %copy-start.2 = (f32[20,320]{1,0:T(8,128)S(1)}, f32[20,320]{1,0:T(8,128)}, u32[]{:S(2)}) copy-start(f32[20,320]{1,0:T(8,128)} %param.17) | copy-start | bytes 76804
  43.2 206.6 %copy-start.3 = (f32[20,320]{1,0:T(8,128)S(1)}, f32[20,320]{1,0:T(8,128)}, u32[]{:S(2)}) copy-start(f32[20,320]{1,0:T(8,128)} %param.16) | copy-start | bytes 76804
Sparse Core Ops, SparseCore 0:
  43.3 203.7 all-reduce.2
